TPU v7x, 32 devices: a whole 2x2x4 slice. The times are simulated.
32 devices in a mesh: depth: 4 (over y, x), screen: 8 (over z, core).
Axes of the slice: x: 2, y: 2, z: 4, core: 2. Of those that a mesh axis runs over, the one named last changes fastest.
Arguments:
- voxel_bins: int32 [32, 256, 2048], P('depth', None, 'screen'), may hold values from 0 to 255
- colors: bfloat16 [3, 256], replicated, may hold values from 0 to 2
- opacity: bfloat16 [256], replicated, may hold values from 0 to 1
- slab_order: int32 [8, 4], replicated, may hold values from 0 to 3, each once within a row
Outputs:
- image: float32 [4, 256, 2048], P(None, ('depth', 'screen'))
Inputs may be any that keep to these rules, and one draw needn't show every extreme that they name: `slab_order`: every row is a permutation of 0 to 3.
All inputs are finite; a program needn't handle non-finite values.
Results may differ from a plain program's by a relative error of at most 0.0003.
Values sent between devices are 32-bit elements; how exact they have to be, the bound alone decides.
A program may use at most 64 MiB of HBM per device.

v0:
```python
import math

import jax
import jax.numpy as jnp
from jax import lax
from jax.sharding import PartitionSpec as P

low_count = 16
extinction = 3.0


def look_up(table_rows, bin_block):
    high_count = table_rows.shape[0] // 4
    low_part = bin_block % low_count
    high_part = bin_block // low_count
    low_onehot = (low_part[None, :] == jnp.arange(low_count, dtype=jnp.int32)[:, None]).astype(
        jnp.bfloat16
    )
    picked = jnp.dot(table_rows, low_onehot, preferred_element_type=jnp.float32)
    picked = picked.reshape(4, high_count, bin_block.shape[0])
    high_match = high_part[None, :] == jnp.arange(high_count, dtype=jnp.int32)[:, None]
    return jnp.sum(jnp.where(high_match[None], picked, 0.0), axis=1)


def render(voxel_bins, table_rows, total_samples):
    samples_here, row_count, col_count = voxel_bins.shape
    pixels = row_count * col_count
    per_step = math.gcd(samples_here, max(1, 131072 // pixels))
    blocks = voxel_bins.reshape(samples_here // per_step, per_step * pixels)
    extinct_rate = extinction / total_samples

    def advance(carried, bin_block):
        passed, color_sum = carried
        values = look_up(table_rows, bin_block).reshape(4, per_step, pixels)
        density = values[3]
        before = jnp.cumsum(density, axis=0) - density
        weight = (1.0 - jnp.exp(-extinct_rate * density)) * jnp.exp(
            -extinct_rate * (passed[None] + before)
        )
        color_sum = color_sum + jnp.sum(weight[None] * values[:3], axis=1)
        return ((passed + jnp.sum(density, axis=0), color_sum), None)

    start = (jnp.zeros((pixels,), jnp.float32), jnp.zeros((3, pixels), jnp.float32))
    (passed, color_sum), ignored = lax.scan(advance, start, blocks)
    final_alpha = 1.0 - jnp.exp(-extinct_rate * passed)
    partial_value = jnp.concatenate([color_sum, final_alpha[None]], axis=0)
    return partial_value.reshape(4, row_count, col_count)


def composite(pieces, places):
    in_front = (places[:, None, :] < places[:, :, None]).astype(jnp.float32)
    clear_log = jnp.log1p(-pieces[:, :, 3])
    front_log = jnp.einsum("tij,jtrw->itrw", in_front, clear_log, precision=lax.Precision.HIGHEST)
    shaded = jnp.sum(pieces[:, :, :3] * jnp.exp(front_log)[:, :, None], axis=0)
    total_alpha = 1.0 - jnp.exp(jnp.sum(clear_log, axis=0))
    merged = jnp.concatenate([shaded, total_alpha[:, None]], axis=1)
    return jnp.transpose(merged, (1, 2, 0, 3))


def local(voxel_bins, colors, opacity, slab_order):
    table = jnp.concatenate([colors, opacity[None]], axis=0)
    table_rows = table.reshape(4 * (table.shape[1] // low_count), low_count)
    depth_count = lax.axis_size("depth")
    total_samples = voxel_bins.shape[0] * depth_count
    partial_value = render(voxel_bins, table_rows, total_samples)
    own_order = lax.dynamic_slice_in_dim(slab_order, lax.axis_index("screen"), 1, 0)
    tile_block = composite(
        lax.all_to_all(partial_value[None], "depth", split_axis=2, concat_axis=0, tiled=True)[
            :, None
        ],
        own_order,
    )[:, :, 0]
    result = lax.all_to_all(tile_block, "screen", split_axis=1, concat_axis=2, tiled=True)
    return result


def solution(mesh):
    placed = (P("depth", None, "screen"), P(), P(), P())
    return jax.shard_map(
        local,
        mesh=mesh,
        in_specs=placed,
        out_specs=P(None, ("depth", "screen"), None),
        check_vma=False,
    )
```

profile of v0, /device:TPU:0, one launch (start us, length us, event | category | flops | bytes accessed | tf_op | source)
XLA Modules:
  0.0 185.4 jit_solution(1392531687887182417)
XLA Ops:
  0.0 4.0 %reshape.163 = s32[4,131072]{1,0:T(4,128)} reshape(s32[8,256,256]{2,1,0:T(8,128)} %param.6) | data formatting | bytes 4194304 | tf_op jit(solution)/shard_map/reshape | solution.py:29
  4.2 141.1 %while.15 = (s32[]{:T(128)}, f32[65536]{0:T(1024)}, f32[3,65536]{1,0:T(4,128)}, s32[4,131072]{1,0:T(4,128)}, bf16[64,16]{0,1:T(8,128)(2,1)S(1)}, /*index=5*/s32[]{:T(128)}, f32[]{:T(128)}, s32[]{:T(128)}) while((s32[]{:T(128)}, f32[65536]{0:T(1024)}, f32[3,65536]{1,0:T(4,128)}, s32[4,131072]{1,0:T(4,128)}, ...), condition=%wide.region_5.6_spmd.clone, body=%wide.region_0.5_spmd.clone.sunk | while | flops 293994496 | bytes 31983784 | solution.py:44
  4.2 3.4 %and_select_fusion.4 = (s32[1,131072]{1,0:T(1,128)S(1)}, s32[1,131072]{1,0:T(1,128)S(1)}) fusion(s32[4,131072]{1,0:T(4,128)} %get-tuple-element.186, s32[]{:T(128)} %get-tuple-element.175), kind=kLoop, calls=%fused_computation.5.clone.1 | loop fusion | flops 1441792 | bytes 1572868 | tf_op jit(solution)/shard_map/while/body/eval_jaxpr/jit(remainder)/select_n | solution.py:14
  7.6 3.8 %and_select_fusion.5 = s32[1,131072]{1,0:T(1,128)S(1)} fusion(s32[1,131072]{1,0:T(1,128)S(1)} %get-tuple-element.163, s32[4,131072]{1,0:T(4,128)} %get-tuple-element.186, s32[]{:T(128)} %get-tuple-element.175), kind=kLoop, calls=%fused_computation.6.clone.1 | loop fusion | flops 1572864 | bytes 1572868 | tf_op jit(solution)/shard_map/while/body/eval_jaxpr/jit(floor_divide)/jit(_where)/select_n | solution.py:15
  12.5 11.0 %select_reduce_fusion.2 = f32[4,131072]{1,0:T(4,128)S(1)} fusion(pred[16,131072]{1,0:T(8,128)(4,1)S(1)} %iota_compare_fusion.4, bf16[64,16]{0,1:T(8,128)(2,1)S(1)} %get-tuple-element.187, s32[131072]{0:T(1024)S(1)} %bitcast.47), kind=kOutput, calls=%fused_computation.clone.1 | convolution fusion | flops 286785536 | bytes 4720640 | tf_op jit(solution)/shard_map/while/body/eval_jaxpr/dot_general | solution.py:19
  33.3 3.9 %multiply_reduce_fusion.2 = f32[3,65536]{1,0:T(4,128)S(1)} fusion(f32[3,2,65536]{2,1,0:T(2,128)} %slice.46, f32[2,65536]{1,0:T(2,128)S(1)} %exponential_multiply_fusion.2), kind=kLoop, calls=%fused_computation.7.clone.1 | loop fusion | flops 589824 | bytes 2883584 | tf_op jit(solution)/shard_map/while/body/eval_jaxpr/reduce_sum | solution.py:40
  38.8 3.4 %and_select_fusion.4 = (s32[1,131072]{1,0:T(1,128)S(1)}, s32[1,131072]{1,0:T(1,128)S(1)}) fusion(s32[4,131072]{1,0:T(4,128)} %get-tuple-element.186, s32[]{:T(128)} %get-tuple-element.175), kind=kLoop, calls=%fused_computation.5.clone.1 | loop fusion | flops 1441792 | bytes 1572868 | tf_op jit(solution)/shard_map/while/body/eval_jaxpr/jit(remainder)/select_n | solution.py:14
  42.2 3.8 %and_select_fusion.5 = s32[1,131072]{1,0:T(1,128)S(1)} fusion(s32[1,131072]{1,0:T(1,128)S(1)} %get-tuple-element.163, s32[4,131072]{1,0:T(4,128)} %get-tuple-element.186, s32[]{:T(128)} %get-tuple-element.175), kind=kLoop, calls=%fused_computation.6.clone.1 | loop fusion | flops 1572864 | bytes 1572868 | tf_op jit(solution)/shard_map/while/body/eval_jaxpr/jit(floor_divide)/jit(_where)/select_n | solution.py:15
  47.0 11.0 %select_reduce_fusion.2 = f32[4,131072]{1,0:T(4,128)S(1)} fusion(pred[16,131072]{1,0:T(8,128)(4,1)S(1)} %iota_compare_fusion.4, bf16[64,16]{0,1:T(8,128)(2,1)S(1)} %get-tuple-element.187, s32[131072]{0:T(1024)S(1)} %bitcast.47), kind=kOutput, calls=%fused_computation.clone.1 | convolution fusion | flops 286785536 | bytes 4720640 | tf_op jit(solution)/shard_map/while/body/eval_jaxpr/dot_general | solution.py:19
  66.0 2.9 %slice.46 = f32[3,2,65536]{2,1,0:T(2,128)} reshape(f32[3,131072]{1,0:T(4,128)S(1)} %bitcast.45) | data formatting | bytes 3145728 | tf_op jit(solution)/shard_map/while/body/eval_jaxpr/slice | solution.py:40
  68.8 3.9 %multiply_reduce_fusion.2 = f32[3,65536]{1,0:T(4,128)S(1)} fusion(f32[3,2,65536]{2,1,0:T(2,128)} %slice.46, f32[2,65536]{1,0:T(2,128)S(1)} %exponential_multiply_fusion.2), kind=kLoop, calls=%fused_computation.7.clone.1 | loop fusion | flops 589824 | bytes 2883584 | tf_op jit(solution)/shard_map/while/body/eval_jaxpr/reduce_sum | solution.py:40
  74.3 3.4 %and_select_fusion.4 = (s32[1,131072]{1,0:T(1,128)S(1)}, s32[1,131072]{1,0:T(1,128)S(1)}) fusion(s32[4,131072]{1,0:T(4,128)} %get-tuple-element.186, s32[]{:T(128)} %get-tuple-element.175), kind=kLoop, calls=%fused_computation.5.clone.1 | loop fusion | flops 1441792 | bytes 1572868 | tf_op jit(solution)/shard_map/while/body/eval_jaxpr/jit(remainder)/select_n | solution.py:14
  77.7 3.8 %and_select_fusion.5 = s32[1,131072]{1,0:T(1,128)S(1)} fusion(s32[1,131072]{1,0:T(1,128)S(1)} %get-tuple-element.163, s32[4,131072]{1,0:T(4,128)} %get-tuple-element.186, s32[]{:T(128)} %get-tuple-element.175), kind=kLoop, calls=%fused_computation.6.clone.1 | loop fusion | flops 1572864 | bytes 1572868 | tf_op jit(solution)/shard_map/while/body/eval_jaxpr/jit(floor_divide)/jit(_where)/select_n | solution.py:15
  82.5 11.0 %select_reduce_fusion.2 = f32[4,131072]{1,0:T(4,128)S(1)} fusion(pred[16,131072]{1,0:T(8,128)(4,1)S(1)} %iota_compare_fusion.4, bf16[64,16]{0,1:T(8,128)(2,1)S(1)} %get-tuple-element.187, s32[131072]{0:T(1024)S(1)} %bitcast.47), kind=kOutput, calls=%fused_computation.clone.1 | convolution fusion | flops 286785536 | bytes 4720640 | tf_op jit(solution)/shard_map/while/body/eval_jaxpr/dot_general | solution.py:19
  101.5 2.9 %slice.46 = f32[3,2,65536]{2,1,0:T(2,128)} reshape(f32[3,131072]{1,0:T(4,128)S(1)} %bitcast.45) | data formatting | bytes 3145728 | tf_op jit(solution)/shard_map/while/body/eval_jaxpr/slice | solution.py:40
  104.3 3.9 %multiply_reduce_fusion.2 = f32[3,65536]{1,0:T(4,128)S(1)} fusion(f32[3,2,65536]{2,1,0:T(2,128)} %slice.46, f32[2,65536]{1,0:T(2,128)S(1)} %exponential_multiply_fusion.2), kind=kLoop, calls=%fused_computation.7.clone.1 | loop fusion | flops 589824 | bytes 2883584 | tf_op jit(solution)/shard_map/while/body/eval_jaxpr/reduce_sum | solution.py:40
  109.8 3.4 %and_select_fusion.4 = (s32[1,131072]{1,0:T(1,128)S(1)}, s32[1,131072]{1,0:T(1,128)S(1)}) fusion(s32[4,131072]{1,0:T(4,128)} %get-tuple-element.186, s32[]{:T(128)} %get-tuple-element.175), kind=kLoop, calls=%fused_computation.5.clone.1 | loop fusion | flops 1441792 | bytes 1572868 | tf_op jit(solution)/shard_map/while/body/eval_jaxpr/jit(remainder)/select_n | solution.py:14
  113.2 3.8 %and_select_fusion.5 = s32[1,131072]{1,0:T(1,128)S(1)} fusion(s32[1,131072]{1,0:T(1,128)S(1)} %get-tuple-element.163, s32[4,131072]{1,0:T(4,128)} %get-tuple-element.186, s32[]{:T(128)} %get-tuple-element.175), kind=kLoop, calls=%fused_computation.6.clone.1 | loop fusion | flops 1572864 | bytes 1572868 | tf_op jit(solution)/shard_map/while/body/eval_jaxpr/jit(floor_divide)/jit(_where)/select_n | solution.py:15
  118.0 11.0 %select_reduce_fusion.2 = f32[4,131072]{1,0:T(4,128)S(1)} fusion(pred[16,131072]{1,0:T(8,128)(4,1)S(1)} %iota_compare_fusion.4, bf16[64,16]{0,1:T(8,128)(2,1)S(1)} %get-tuple-element.187, s32[131072]{0:T(1024)S(1)} %bitcast.47), kind=kOutput, calls=%fused_computation.clone.1 | convolution fusion | flops 286785536 | bytes 4720640 | tf_op jit(solution)/shard_map/while/body/eval_jaxpr/dot_general | solution.py:19
  137.0 2.9 %slice.46 = f32[3,2,65536]{2,1,0:T(2,128)} reshape(f32[3,131072]{1,0:T(4,128)S(1)} %bitcast.45) | data formatting | bytes 3145728 | tf_op jit(solution)/shard_map/while/body/eval_jaxpr/slice | solution.py:40
  139.8 3.9 %multiply_reduce_fusion.2 = f32[3,65536]{1,0:T(4,128)S(1)} fusion(f32[3,2,65536]{2,1,0:T(2,128)} %slice.46, f32[2,65536]{1,0:T(2,128)S(1)} %exponential_multiply_fusion.2), kind=kLoop, calls=%fused_computation.7.clone.1 | loop fusion | flops 589824 | bytes 2883584 | tf_op jit(solution)/shard_map/while/body/eval_jaxpr/reduce_sum | solution.py:40
  149.0 5.2 %all-to-all-start = ((f32[1,4,256,256]{3,1,0,2:T(4,128)}), f32[1,4,256,256]{3,1,0,2:T(4,128)S(1)}, u32[]{:S(2)}, u32[]{:S(2)}) async-start(f32[1,4,256,256]{3,1,0,2:T(4,128)} %pad_maximum_fusion), calls=%async_computation | async-start | bytes 2097152 | tf_op jit(solution)/shard_map/all_to_all | solution.py:68
  154.4 13.4 %all-to-all-done = f32[1,4,256,256]{3,1,0,2:T(4,128)S(1)} async-done(((f32[1,4,256,256]{3,1,0,2:T(4,128)}), f32[1,4,256,256]{3,1,0,2:T(4,128)S(1)}, u32[]{:S(2)}, u32[]{:S(2)}) %all-to-all-start) | async-done | bytes 1048608 | tf_op jit(solution)/shard_map/all_to_all | solution.py:68
  170.2 14.4 %all_to_all.33 = f32[4,64,256]{2,0,1:T(4,128)S(1)} all-to-all(f32[4,64,256]{2,0,1:T(4,128)S(1)} %copy.19), channel_id=1, replica_groups=mesh['depth'=4,'screen'=8] {'screen'}, dimensions={1} | all-to-all | bytes 524288 | tf_op jit(solution)/shard_map/all_to_all | solution.py:73
  (72 shorter events, 51.1 us)
Async XLA Ops:
  0.0 154.2 %copy-start = (s32[8,4]{0,1:T(4,128)S(1)}, s32[8,4]{0,1:T(4,128)}, u32[]{:S(2)}) copy-start(s32[8,4]{0,1:T(4,128)} %param.9) | copy-start | bytes 388
  0.0 4.0 %copy-start.4 = (bf16[256]{0:T(256)(128)(2,1)S(1)}, bf16[256]{0:T(256)(128)(2,1)}, u32[]{:S(2)}) copy-start(bf16[256]{0:T(256)(128)(2,1)} %param.8) | copy-start | bytes 1540
  0.0 4.0 %copy-start.3 = (bf16[3,256]{1,0:T(4,128)(2,1)S(1)}, bf16[3,256]{1,0:T(4,128)(2,1)}, u32[]{:S(2)}) copy-start(bf16[3,256]{1,0:T(4,128)(2,1)} %param.7) | copy-start | bytes 4612
  33.3 3.9 %copy-start.1 = (f32[3,65536]{1,0:T(4,128)S(1)}, f32[3,65536]{1,0:T(4,128)}, u32[]{:S(2)}) copy-start(f32[3,65536]{1,0:T(4,128)} %get-tuple-element.177) | copy-start | bytes 2359300 | tf_op jit(solution)/shard_map/while
  37.8 1.0 copy-start.2
  68.8 3.9 %copy-start.1 = (f32[3,65536]{1,0:T(4,128)S(1)}, f32[3,65536]{1,0:T(4,128)}, u32[]{:S(2)}) copy-start(f32[3,65536]{1,0:T(4,128)} %get-tuple-element.177) | copy-start | bytes 2359300 | tf_op jit(solution)/shard_map/while
  73.4 1.0 copy-start.2
  104.3 3.9 %copy-start.1 = (f32[3,65536]{1,0:T(4,128)S(1)}, f32[3,65536]{1,0:T(4,128)}, u32[]{:S(2)}) copy-start(f32[3,65536]{1,0:T(4,128)} %get-tuple-element.177) | copy-start | bytes 2359300 | tf_op jit(solution)/shard_map/while
  108.9 1.0 copy-start.2
  139.8 3.9 %copy-start.1 = (f32[3,65536]{1,0:T(4,128)S(1)}, f32[3,65536]{1,0:T(4,128)}, u32[]{:S(2)}) copy-start(f32[3,65536]{1,0:T(4,128)} %get-tuple-element.177) | copy-start | bytes 2359300 | tf_op jit(solution)/shard_map/while
  144.4 1.0 copy-start.2
  149.0 18.8 %all-to-all-start = ((f32[1,4,256,256]{3,1,0,2:T(4,128)}), f32[1,4,256,256]{3,1,0,2:T(4,128)S(1)}, u32[]{:S(2)}, u32[]{:S(2)}) async-start(f32[1,4,256,256]{3,1,0,2:T(4,128)} %pad_maximum_fusion), calls=%async_computation | async-start | bytes 2097152 | tf_op jit(solution)/shard_map/all_to_all | solution.py:68
where the time goes:
time: 186 us; the launch traced here: 185 us
  other arithmetic  78.4 us (42%)
  matrix products  44.8 us (24%)
  local copies, waits for them, and re-layouts  28.7 us (15%)
  blocking collectives  14.4 us (8%)
  waiting for transfers between devices  13.4 us (7%)
  starting transfers between devices  5.19 us (3%)
    dot_general x4, matrix products, look_up(): picked = jnp.dot(table_rows, low_onehot, preferred_element_type=jnp.float32)  44.2 us
    reduce_sum x4, other arithmetic, advance(): color_sum = color_sum + jnp.sum(weight[None] * values[:3], axis=1)  15.5 us
    select_n x4, other arithmetic, look_up(): high_part = bin_block // low_count  15 us
    all_to_all x1, blocking collectives, local(): lax.all_to_all(tile_block, 'screen', split_axis=1, concat_axis=2, tiled=T...  14.4 us
    select_n x4, other arithmetic, look_up(): low_part = bin_block % low_count  13.5 us
    all_to_all x1, waiting for transfers between devices, local(): lax.all_to_all(partial_value[None], 'depth', split_axis=2, concat_axis=0,...  13.4 us
    slice x4, local copies, waits for them, and re-layouts, advance(): color_sum = color_sum + jnp.sum(weight[None] * values[:3], axis=1)  11.4 us
    another operation x4, other arithmetic, advance(): before = jnp.cumsum(density, axis=0) - density  7.29 us
  transfers between devices with their start and end apart: 1, of which 1 were waited for; matrix products, arithmetic and copies ran while one was open for 0% of the time, Pallas kernels for 0%

commit v1 on v0

v1 whole, which is shorter than its diff:
```python
import functools

import jax
import jax.numpy as jnp
from jax import lax
from jax.experimental import pallas as pl
from jax.experimental.pallas import tpu as pltpu
from jax.sharding import PartitionSpec as P

extinction = 3.0
lanes = 128
MESH = pl.DeviceIdType.MESH


def flip(index, mask):
    result = index
    bit = 1
    while bit <= mask:
        if mask & bit:
            result = result + bit * (1 - 2 * lax.rem(lax.div(index, bit), 2))
        bit *= 2
    return result


def kernel(
    sizes,
    order_ref,
    bins_hbm,
    colors_ref,
    opacity_ref,
    out_ref,
    bins,
    sent,
    own,
    arrived,
    merged,
    bins_sem,
    send_sem,
    recv_sem,
    row_send_sem,
    row_recv_sem,
):
    depth_count, tile_count, samples, unit_rows, units, owners, rows_each, cols, rate = sizes
    depth = lax.axis_index("depth")
    tile = lax.axis_index("screen")
    own_unit = lax.div(tile, owners)
    own_place = lax.rem(tile, owners)
    steps = list(range(units - 1, -1, -1))
    peers = [depth_count - 1] + list(range(1, depth_count - 1)) + [0]

    barrier = pltpu.get_barrier_semaphore()
    for mask in range(1, depth_count):
        pl.semaphore_signal(
            barrier, inc=1, device_id=(flip(depth, mask), tile), device_id_type=MESH
        )
    for mask in range(1, tile_count):
        pl.semaphore_signal(
            barrier, inc=1, device_id=(depth, flip(tile, mask)), device_id_type=MESH
        )

    def fetch(step, mask):
        row = (flip(depth, mask) * units + flip(own_unit, step)) * unit_rows
        row = pl.multiple_of(row, unit_rows)
        return pltpu.make_async_copy(
            bins_hbm.at[:, pl.ds(row, unit_rows), :],
            bins.at[step, mask],
            bins_sem.at[step, mask],
        )

    for step in steps:
        for mask in peers:
            if mask:
                fetch(step, mask).start()
    for step in steps:
        fetch(step, 0).start()

    density = opacity_ref[...].astype(jnp.float32)
    weight = 1.0 - jnp.exp(-rate * density)
    shades = weight * colors_ref[...].astype(jnp.float32)
    table = [shades[c : c + 1] for c in range(3)] + [weight]
    bin_count = weight.shape[1]
    parts = [
        [jnp.broadcast_to(row[:, at : at + lanes], (8, lanes)) for at in range(0, bin_count, lanes)]
        for row in table
    ]

    def march(step, mask, target):
        for row in range(0, unit_rows, 8):
            for col in range(0, cols, lanes):
                clear = None
                total = None
                for j in range(samples):
                    index = bins[step, mask, j, row : row + 8, col : col + lanes]
                    low = lax.rem(index, lanes) if lanes & (lanes - 1) else index & (lanes - 1)
                    values = []
                    for part in parts:
                        value = jnp.take_along_axis(part[0], low, axis=1, mode="promise_in_bounds")
                        for n in range(1, len(part)):
                            other = jnp.take_along_axis(
                                part[n], low, axis=1, mode="promise_in_bounds"
                            )
                            value = jnp.where(index >= n * lanes, other, value)
                        values.append(value)
                    if total is None:
                        total = values
                        clear = 1.0 - values[3]
                    else:
                        seen = clear * values[3]
                        total = [t + clear * v for t, v in zip(total[:3], values[:3])] + [
                            total[3] + seen
                        ]
                        clear = clear - seen
                for c in range(4):
                    target[c, row : row + 8, col : col + lanes] = total[c]

    def send(step, mask):
        return pltpu.make_async_remote_copy(
            src_ref=sent.at[step, mask - 1],
            dst_ref=arrived.at[step, mask - 1],
            send_sem=send_sem.at[step, mask - 1],
            recv_sem=recv_sem.at[step, mask - 1],
            device_id=(flip(depth, mask), tile),
            device_id_type=MESH,
        )

    def send_row(step, low):
        mask = step * owners + low
        place = flip(own_place, low)
        there = pl.ds(pl.multiple_of(tile * cols, lanes), cols)
        return pltpu.make_async_remote_copy(
            src_ref=merged.at[step, place],
            dst_ref=out_ref.at[:, :, there],
            send_sem=row_send_sem.at[mask],
            recv_sem=row_recv_sem.at[mask],
            device_id=(depth, flip(tile, mask)),
            device_id_type=MESH,
        )

    def take_row(mask):
        here = pl.ds(pl.multiple_of(flip(tile, mask) * cols, lanes), cols)
        return pltpu.make_async_remote_copy(
            src_ref=merged.at[0, 0],
            dst_ref=out_ref.at[:, :, here],
            send_sem=row_send_sem.at[mask],
            recv_sem=row_recv_sem.at[mask],
            device_id=(depth, flip(tile, mask)),
            device_id_type=MESH,
        )

    for step in steps:
        for mask in peers:
            if mask:
                fetch(step, mask).wait()
                march(step, mask, sent.at[step, mask - 1])
        if step == steps[0]:
            pl.semaphore_wait(barrier, depth_count + tile_count - 2)
        for mask in peers:
            if mask:
                send(step, mask).start()
    for step in steps:
        fetch(step, 0).wait()
        march(step, 0, own.at[step])

    place_of = [order_ref[tile, flip(depth, mask)] for mask in range(depth_count)]
    ahead = [
        [jnp.where(place_of[j] < place_of[i], 1.0, 0.0) for j in range(depth_count)]
        for i in range(depth_count)
    ]

    for step in steps:
        for mask in peers:
            if mask:
                send(step, mask).wait_recv()
        for row in range(0, unit_rows, 8):
            for col in range(0, cols, lanes):
                window = (slice(row, row + 8), slice(col, col + lanes))
                pieces = [
                    own[(step, slice(None)) + window]
                    if mask == 0
                    else arrived[(step, mask - 1, slice(None)) + window]
                    for mask in range(depth_count)
                ]
                total = None
                for i in range(depth_count):
                    front = None
                    for j in range(depth_count):
                        if j != i:
                            passed = 1.0 - ahead[i][j] * pieces[j][3]
                            front = passed if front is None else front * passed
                    lit = [pieces[i][c] if front is None else pieces[i][c] * front for c in range(4)]
                    total = lit if total is None else [t + v for t, v in zip(total, lit)]
                for c in range(4):
                    if owners == 1:
                        merged[step, 0, c, row : row + 8, col : col + lanes] = total[c]
                    else:
                        for place in range(owners):
                            merged[step, place, c, :, col : col + lanes] = total[c][
                                place * rows_each : (place + 1) * rows_each
                            ]
        for low in range(owners - 1, -1, -1):
            if step * owners + low:
                send_row(step, low).start()
            else:
                here = pl.ds(pl.multiple_of(tile * cols, lanes), cols)
                out_ref[:, :, here] = merged[step, own_place]

    for mask in range(tile_count - 1, 0, -1):
        take_row(mask).wait_recv()
    for step in steps:
        for mask in range(1, depth_count):
            send(step, mask).wait_send()
    for mask in range(1, tile_count):
        send_row(mask // owners, mask % owners).wait_send()


def local(voxel_bins, colors, opacity, slab_order):
    depth_count = lax.axis_size("depth")
    tile_count = lax.axis_size("screen")
    samples, row_count, cols = voxel_bins.shape
    rows_each = row_count // (depth_count * tile_count)
    unit_rows = max(8, rows_each)
    owners = unit_rows // rows_each
    units = tile_count // owners
    rate = extinction / (samples * depth_count)
    sizes = (depth_count, tile_count, samples, unit_rows, units, owners, rows_each, cols, rate)
    others = depth_count - 1
    vmem = pl.BlockSpec(memory_space=pltpu.VMEM)
    return pl.pallas_call(
        functools.partial(kernel, sizes),
        out_shape=jax.ShapeDtypeStruct((4, rows_each, cols * tile_count), jnp.float32),
        in_specs=[
            pl.BlockSpec(memory_space=pltpu.SMEM),
            pl.BlockSpec(memory_space=pl.ANY),
            vmem,
            vmem,
        ],
        out_specs=vmem,
        scratch_shapes=[
            pltpu.VMEM((units, depth_count, samples, unit_rows, cols), jnp.int32),
            pltpu.VMEM((units, others, 4, unit_rows, cols), jnp.float32),
            pltpu.VMEM((units, 4, unit_rows, cols), jnp.float32),
            pltpu.VMEM((units, others, 4, unit_rows, cols), jnp.float32),
            pltpu.VMEM((units, owners, 4, rows_each, cols), jnp.float32),
            pltpu.SemaphoreType.DMA((units, depth_count)),
            pltpu.SemaphoreType.DMA((units, others)),
            pltpu.SemaphoreType.DMA((units, others)),
            pltpu.SemaphoreType.DMA((tile_count,)),
            pltpu.SemaphoreType.DMA((tile_count,)),
        ],
        compiler_params=pltpu.CompilerParams(collective_id=0, has_side_effects=True),
    )(slab_order, voxel_bins, colors, opacity[None])


def solution(mesh):
    placed = (P("depth", None, "screen"), P(), P(), P())
    return jax.shard_map(
        local,
        mesh=mesh,
        in_specs=placed,
        out_specs=P(None, ("depth", "screen"), None),
        check_vma=False,
    )
```

time: 186 us -> 26.9 us (0.14)
  other arithmetic: 78.4 us -> 0 us
  matrix products: 44.8 us -> 0 us
  local copies, waits for them, and re-layouts: 28.7 us -> 4.25 us
  Pallas kernels: 0 us -> 22.4 us
  blocking collectives: 14.4 us -> 0 us
  waiting for transfers between devices: 13.4 us -> 0 us
  starting transfers between devices: 5.19 us -> 0 us
    dot_general x5 -> x0, matrix products: 44.8 us -> none  [the longest x4 44.2 us: look_up(): picked = jnp.dot(table_rows, low_onehot, preferred_element_type=jnp.float32)]
    select_n x8 -> x0, other arithmetic: 28.5 us -> none  [the longest x4 15 us: look_up(): high_part = bin_block // low_count]
    pallas_call x0 -> x1, Pallas kernels: none -> 22.4 us  [local(): pl.pallas_call(functools.partial(kernel, sizes), out_shape=jax.ShapeDtype...]
    reduce_sum x10 -> x0, other arithmetic: 18.9 us -> none  [the longest x4 15.5 us: advance(): color_sum = color_sum + jnp.sum(weight[None] * values[:3], axis=1)]
    slice x8 -> x0, local copies, waits for them, and re-layouts: 17.7 us -> none  [the longest x4 11.4 us: advance(): color_sum = color_sum + jnp.sum(weight[None] * values[:3], axis=1)]
    all_to_all x1 -> x0, blocking collectives: 14.4 us -> none  [local(): lax.all_to_all(tile_block, 'screen', split_axis=1, concat_axis=2, tiled=T...]
    all_to_all x1 -> x0, waiting for transfers between devices: 13.4 us -> none  [local(): lax.all_to_all(partial_value[None], 'depth', split_axis=2, concat_axis=0,...]
    add x8 -> x0, other arithmetic: 8.45 us -> none  [the longest x4 5.98 us: advance(): return ((passed + jnp.sum(density, axis=0), color_sum), None)]
  transfers between devices with their start and end apart: 1 -> 0, of which waited for: 1 -> 0; matrix products, arithmetic and copies ran while one was open for 0% -> 0% of each run, Pallas kernels for 0% -> 0%
where the time goes in v1:
time: 26.9 us; the launch traced here: 26.7 us
  Pallas kernels  22.4 us (83%)
  local copies, waits for them, and re-layouts  4.25 us (16%)
    pallas_call x1, Pallas kernels, local(): pl.pallas_call(functools.partial(kernel, sizes), out_shape=jax.ShapeDtype...  22.4 us
    unnamed x2, local copies, waits for them, and re-layouts  3.02 us
    broadcast_in_dim x1, local copies, waits for them, and re-layouts, local(): opacity[None]  1.23 us

profile of v1, /device:TPU:0, one launch (start us, length us, event | category | flops | bytes accessed | tf_op | source)
XLA Modules:
  0.0 26.7 jit_solution(1095702385367951440)
XLA Ops:
  0.0 1.2 %broadcast_in_dim.3.opacity_ref = bf16[1,256]{1,0:T(2,128)(2,1)} reshape(bf16[256]{0:T(256)(128)(2,1)} %param.6) | data formatting | bytes 1024 | tf_op jit(solution)/shard_map/broadcast_in_dim | solution.py:251
  1.2 1.3 %copy.5.order_ref = s32[8,4]{1,0:T(8,128)} copy(s32[8,4]{0,1:T(4,128)} %param.7) | data formatting | bytes 256 | tf_op args[3]
  2.6 22.4 %shard_map.46 = f32[4,8,2048]{2,1,0:T(8,128)} custom-call(s32[8,4]{1,0:T(8,128)} %copy.5.order_ref, s32[8,256,256]{2,1,0:T(8,128)} %bins_hbm.1, bf16[3,256]{1,0:T(4,128)(2,1)} %colors_ref.1, bf16[1,256]{1,0:T(2,128)(2,1)} %broadcast_in_dim.3.opacity_ref), custom_call_target="tpu_custom_call" | custom-call | tf_op jit(solution)/shard_map/pallas_call | solution.py:228
  25.0 1.7 %copy.7 = f32[4,8,2048]{2,1,0:T(8,128)} copy(f32[4,8,2048]{2,1,0:T(8,128)} %shard_map.46) | data formatting | bytes 524288

commit v2 on v1

--- a/solution.py
+++ b/solution.py
@@ -74,7 +74,7 @@
     for step in steps:
         fetch(step, 0).start()
 
-    density = opacity_ref[...].astype(jnp.float32)
+    density = opacity_ref[...].astype(jnp.float32).reshape(1, -1)
     weight = 1.0 - jnp.exp(-rate * density)
     shades = weight * colors_ref[...].astype(jnp.float32)
     table = [shades[c : c + 1] for c in range(3)] + [weight]
@@ -161,7 +161,7 @@
         fetch(step, 0).wait()
         march(step, 0, own.at[step])
 
-    place_of = [order_ref[tile, flip(depth, mask)] for mask in range(depth_count)]
+    place_of = [order_ref[flip(depth, mask), tile] for mask in range(depth_count)]
     ahead = [
         [jnp.where(place_of[j] < place_of[i], 1.0, 0.0) for j in range(depth_count)]
         for i in range(depth_count)
@@ -227,7 +227,7 @@
     vmem = pl.BlockSpec(memory_space=pltpu.VMEM)
     return pl.pallas_call(
         functools.partial(kernel, sizes),
-        out_shape=jax.ShapeDtypeStruct((4, rows_each, cols * tile_count), jnp.float32),
+        out_shape=pltpu.VMEM((4, rows_each, cols * tile_count), jnp.float32),
         in_specs=[
             pl.BlockSpec(memory_space=pltpu.SMEM),
             pl.BlockSpec(memory_space=pl.ANY),
@@ -248,7 +248,7 @@
             pltpu.SemaphoreType.DMA((tile_count,)),
         ],
         compiler_params=pltpu.CompilerParams(collective_id=0, has_side_effects=True),
-    )(slab_order, voxel_bins, colors, opacity[None])
+    )(slab_order.T, voxel_bins, colors, opacity)
 
 
 def solution(mesh):

time: 26.9 us -> 22.6 us (0.84)
  local copies, waits for them, and re-layouts: 4.25 us -> 0.71 us
  Pallas kernels: 22.4 us -> 21.7 us
    unnamed x2 -> x1, local copies, waits for them, and re-layouts: 3.02 us -> 0.71 us
    broadcast_in_dim x1 -> x0, local copies, waits for them, and re-layouts: 1.23 us -> none  [local(): opacity[None]]
    pallas_call x1, Pallas kernels: 22.4 us -> 21.7 us  [local(): pl.pallas_call(functools.partial(kernel, sizes), out_shape=pltpu.VMEM((4,...]
where the time goes in v2:
time: 22.6 us; the launch traced here: 22.4 us
  Pallas kernels  21.7 us (96%)
  local copies, waits for them, and re-layouts  0.71 us (3%)
    pallas_call x1, Pallas kernels, local(): pl.pallas_call(functools.partial(kernel, sizes), out_shape=pltpu.VMEM((4,...  21.7 us
    unnamed x1, local copies, waits for them, and re-layouts  0.71 us

profile of v2, /device:TPU:0, one launch (start us, length us, event | category | flops | bytes accessed | tf_op | source)
XLA Modules:
  0.0 22.4 jit_solution(10163594230896413528)
XLA Ops:
  0.0 21.7 %shard_map.46 = f32[4,8,2048]{2,1,0:T(8,128)S(1)} custom-call(s32[4,8]{1,0:T(4,128)} %bitcast.1, s32[8,256,256]{2,1,0:T(8,128)} %bins_hbm.1, bf16[3,256]{1,0:T(4,128)(2,1)} %colors_ref.1, bf16[256]{0:T(256)(128)(2,1)} %opacity_ref.1), custom_call_target="tpu_custom_call" | custom-call | tf_op jit(solution)/shard_map/pallas_call | solution.py:228
  21.7 0.7 %copy.6 = f32[4,8,2048]{2,1,0:T(8,128)} copy(f32[4,8,2048]{2,1,0:T(8,128)S(1)} %shard_map.46) | data formatting | bytes 524288

commit v3 on v2

--- a/solution.py
+++ b/solution.py
@@ -12,12 +12,17 @@
 MESH = pl.DeviceIdType.MESH
 
 
-def flip(index, mask):
+def flip(index, mask, count):
     result = index
     bit = 1
-    while bit <= mask:
-        if mask & bit:
-            result = result + bit * (1 - 2 * lax.rem(lax.div(index, bit), 2))
+    while bit < count:
+        if isinstance(mask, int):
+            if mask & bit:
+                result = result + bit * (1 - 2 * lax.rem(lax.div(index, bit), 2))
+        else:
+            mine = lax.rem(lax.div(index, bit), 2)
+            other = lax.rem(lax.div(mask, bit), 2)
+            result = result + bit * other * (1 - 2 * mine)
         bit *= 2
     return result
 
@@ -51,15 +56,15 @@
     barrier = pltpu.get_barrier_semaphore()
     for mask in range(1, depth_count):
         pl.semaphore_signal(
-            barrier, inc=1, device_id=(flip(depth, mask), tile), device_id_type=MESH
+            barrier, inc=1, device_id=(flip(depth, mask, depth_count), tile), device_id_type=MESH
         )
     for mask in range(1, tile_count):
         pl.semaphore_signal(
-            barrier, inc=1, device_id=(depth, flip(tile, mask)), device_id_type=MESH
+            barrier, inc=1, device_id=(depth, flip(tile, mask, tile_count)), device_id_type=MESH
         )
 
     def fetch(step, mask):
-        row = (flip(depth, mask) * units + flip(own_unit, step)) * unit_rows
+        row = (flip(depth, mask, depth_count) * units + flip(own_unit, step, units)) * unit_rows
         row = pl.multiple_of(row, unit_rows)
         return pltpu.make_async_copy(
             bins_hbm.at[:, pl.ds(row, unit_rows), :],
@@ -119,55 +124,68 @@
             dst_ref=arrived.at[step, mask - 1],
             send_sem=send_sem.at[step, mask - 1],
             recv_sem=recv_sem.at[step, mask - 1],
-            device_id=(flip(depth, mask), tile),
+            device_id=(flip(depth, mask, depth_count), tile),
             device_id_type=MESH,
         )
 
     def send_row(step, low):
         mask = step * owners + low
-        place = flip(own_place, low)
+        place = flip(own_place, low, owners)
         there = pl.ds(pl.multiple_of(tile * cols, lanes), cols)
         return pltpu.make_async_remote_copy(
             src_ref=merged.at[step, place],
             dst_ref=out_ref.at[:, :, there],
             send_sem=row_send_sem.at[mask],
             recv_sem=row_recv_sem.at[mask],
-            device_id=(depth, flip(tile, mask)),
+            device_id=(depth, flip(tile, mask, tile_count)),
             device_id_type=MESH,
         )
 
     def take_row(mask):
-        here = pl.ds(pl.multiple_of(flip(tile, mask) * cols, lanes), cols)
+        here = pl.ds(pl.multiple_of(flip(tile, mask, tile_count) * cols, lanes), cols)
         return pltpu.make_async_remote_copy(
             src_ref=merged.at[0, 0],
             dst_ref=out_ref.at[:, :, here],
             send_sem=row_send_sem.at[mask],
             recv_sem=row_recv_sem.at[mask],
-            device_id=(depth, flip(tile, mask)),
+            device_id=(depth, flip(tile, mask, tile_count)),
             device_id_type=MESH,
         )
 
-    for step in steps:
+    def feed(n, carry):
+        step = units - 1 - n
         for mask in peers:
             if mask:
                 fetch(step, mask).wait()
                 march(step, mask, sent.at[step, mask - 1])
-        if step == steps[0]:
+
+        @pl.when(n == 0)
+        def _():
             pl.semaphore_wait(barrier, depth_count + tile_count - 2)
+
         for mask in peers:
             if mask:
                 send(step, mask).start()
-    for step in steps:
+        return carry
+
+    lax.fori_loop(0, units, feed, 0)
+
+    def keep(n, carry):
+        step = units - 1 - n
         fetch(step, 0).wait()
         march(step, 0, own.at[step])
-
-    place_of = [order_ref[flip(depth, mask), tile] for mask in range(depth_count)]
+        return carry
+
+    lax.fori_loop(0, units, keep, 0)
+
+    place_of = [order_ref[flip(depth, mask, depth_count), tile] for mask in range(depth_count)]
     ahead = [
         [jnp.where(place_of[j] < place_of[i], 1.0, 0.0) for j in range(depth_count)]
         for i in range(depth_count)
     ]
 
-    for step in steps:
+    def blend(n, carry):
+        step = units - 1 - n
         for mask in peers:
             if mask:
                 send(step, mask).wait_recv()
@@ -197,12 +215,18 @@
                             merged[step, place, c, :, col : col + lanes] = total[c][
                                 place * rows_each : (place + 1) * rows_each
                             ]
-        for low in range(owners - 1, -1, -1):
-            if step * owners + low:
-                send_row(step, low).start()
-            else:
-                here = pl.ds(pl.multiple_of(tile * cols, lanes), cols)
-                out_ref[:, :, here] = merged[step, own_place]
+        for low in range(owners - 1, 0, -1):
+            send_row(step, low).start()
+
+        @pl.when(step > 0)
+        def _():
+            send_row(step, 0).start()
+
+        return carry
+
+    lax.fori_loop(0, units, blend, 0)
+    here = pl.ds(pl.multiple_of(tile * cols, lanes), cols)
+    out_ref[:, :, here] = merged[0, own_place]
 
     for mask in range(tile_count - 1, 0, -1):
         take_row(mask).wait_recv()

time: 22.6 us -> 22.7 us (level)
  no operation moved by 1% of the time
where the time goes in v3:
time: 22.7 us; the launch traced here: 22.5 us
  Pallas kernels  21.8 us (96%)
  local copies, waits for them, and re-layouts  0.71 us (3%)
    pallas_call x1, Pallas kernels, local(): pl.pallas_call(functools.partial(kernel, sizes), out_shape=pltpu.VMEM((4,...  21.8 us
    unnamed x1, local copies, waits for them, and re-layouts  0.71 us

profile of v3, /device:TPU:0, one launch (start us, length us, event | category | flops | bytes accessed | tf_op | source)
XLA Modules:
  0.0 22.5 jit_solution(3972619555357006384)
XLA Ops:
  0.0 21.8 %shard_map.46 = f32[4,8,2048]{2,1,0:T(8,128)S(1)} custom-call(s32[4,8]{1,0:T(4,128)} %bitcast.1, s32[8,256,256]{2,1,0:T(8,128)} %bins_hbm.1, bf16[3,256]{1,0:T(4,128)(2,1)} %colors_ref.1, bf16[256]{0:T(256)(128)(2,1)} %opacity_ref.1), custom_call_target="tpu_custom_call" | custom-call | tf_op jit(solution)/shard_map/pallas_call | solution.py:252
  21.8 0.7 %copy.6 = f32[4,8,2048]{2,1,0:T(8,128)} copy(f32[4,8,2048]{2,1,0:T(8,128)S(1)} %shard_map.46) | data formatting | bytes 524288

commit v4 on v3

--- a/solution.py
+++ b/solution.py
@@ -44,6 +44,8 @@
     recv_sem,
     row_send_sem,
     row_recv_sem,
+    ready_sem,
+    go_sem,
 ):
     depth_count, tile_count, samples, unit_rows, units, owners, rows_each, cols, rate = sizes
     depth = lax.axis_index("depth")
@@ -54,14 +56,41 @@
     peers = [depth_count - 1] + list(range(1, depth_count - 1)) + [0]
 
     barrier = pltpu.get_barrier_semaphore()
+    hub = depth == 0
     for mask in range(1, depth_count):
-        pl.semaphore_signal(
-            barrier, inc=1, device_id=(flip(depth, mask, depth_count), tile), device_id_type=MESH
-        )
-    for mask in range(1, tile_count):
-        pl.semaphore_signal(
-            barrier, inc=1, device_id=(depth, flip(tile, mask, tile_count)), device_id_type=MESH
-        )
+        peer = flip(depth, mask, depth_count)
+
+        @pl.when(peer != 0)
+        def _():
+            pl.semaphore_signal(barrier, inc=1, device_id=(peer, tile), device_id_type=MESH)
+
+    def meet_depth():
+        @pl.when(jnp.logical_not(hub))
+        def _():
+            pl.semaphore_wait(barrier, depth_count - 1)
+            pl.semaphore_signal(ready_sem, inc=1, device_id=(0, tile), device_id_type=MESH)
+
+        @pl.when(hub)
+        def _():
+            pl.semaphore_wait(ready_sem, depth_count - 1)
+            for mask in range(1, tile_count):
+                pl.semaphore_signal(
+                    barrier,
+                    inc=1,
+                    device_id=(0, flip(tile, mask, tile_count)),
+                    device_id_type=MESH,
+                )
+
+    def meet_tiles():
+        @pl.when(hub)
+        def _():
+            pl.semaphore_wait(barrier, tile_count - 1)
+            for mask in range(1, depth_count):
+                pl.semaphore_signal(go_sem, inc=1, device_id=(mask, tile), device_id_type=MESH)
+
+        @pl.when(jnp.logical_not(hub))
+        def _():
+            pl.semaphore_wait(go_sem, 1)
 
     def fetch(step, mask):
         row = (flip(depth, mask, depth_count) * units + flip(own_unit, step, units)) * unit_rows
@@ -161,7 +190,7 @@
 
         @pl.when(n == 0)
         def _():
-            pl.semaphore_wait(barrier, depth_count + tile_count - 2)
+            meet_depth()
 
         for mask in peers:
             if mask:
@@ -177,6 +206,7 @@
         return carry
 
     lax.fori_loop(0, units, keep, 0)
+    meet_tiles()
 
     place_of = [order_ref[flip(depth, mask, depth_count), tile] for mask in range(depth_count)]
     ahead = [
@@ -270,6 +300,8 @@
             pltpu.SemaphoreType.DMA((units, others)),
             pltpu.SemaphoreType.DMA((tile_count,)),
             pltpu.SemaphoreType.DMA((tile_count,)),
+            pltpu.SemaphoreType.REGULAR,
+            pltpu.SemaphoreType.REGULAR,
         ],
         compiler_params=pltpu.CompilerParams(collective_id=0, has_side_effects=True),
     )(slab_order.T, voxel_bins, colors, opacity)

time: 22.7 us -> 24.4 us (1.075)
  Pallas kernels: 21.8 us -> 23.5 us
    pallas_call x1, Pallas kernels: 21.8 us -> 23.5 us  [local(): pl.pallas_call(functools.partial(kernel, sizes), out_shape=pltpu.VMEM((4,...]
where the time goes in v4:
time: 24.4 us; the launch traced here: 24.2 us
  Pallas kernels  23.5 us (96%)
  local copies, waits for them, and re-layouts  0.71 us (3%)
    pallas_call x1, Pallas kernels, local(): pl.pallas_call(functools.partial(kernel, sizes), out_shape=pltpu.VMEM((4,...  23.5 us
    unnamed x1, local copies, waits for them, and re-layouts  0.71 us

profile of v4, /device:TPU:0, one launch (start us, length us, event | category | flops | bytes accessed | tf_op | source)
XLA Modules:
  0.0 24.2 jit_solution(3934985537627947177)
XLA Ops:
  0.0 23.5 %shard_map.46 = f32[4,8,2048]{2,1,0:T(8,128)S(1)} custom-call(s32[4,8]{1,0:T(4,128)} %bitcast.1, s32[8,256,256]{2,1,0:T(8,128)} %bins_hbm.1, bf16[3,256]{1,0:T(4,128)(2,1)} %colors_ref.1, bf16[256]{0:T(256)(128)(2,1)} %opacity_ref.1), custom_call_target="tpu_custom_call" | custom-call | tf_op jit(solution)/shard_map/pallas_call | solution.py:282
  23.5 0.7 %copy.6 = f32[4,8,2048]{2,1,0:T(8,128)} copy(f32[4,8,2048]{2,1,0:T(8,128)S(1)} %shard_map.46) | data formatting | bytes 524288

commit v5 on v4

--- a/solution.py
+++ b/solution.py
@@ -181,7 +181,7 @@
             device_id_type=MESH,
         )
 
-    def feed(n, carry):
+    def feed(n):
         step = units - 1 - n
         for mask in peers:
             if mask:
@@ -195,18 +195,6 @@
         for mask in peers:
             if mask:
                 send(step, mask).start()
-        return carry
-
-    lax.fori_loop(0, units, feed, 0)
-
-    def keep(n, carry):
-        step = units - 1 - n
-        fetch(step, 0).wait()
-        march(step, 0, own.at[step])
-        return carry
-
-    lax.fori_loop(0, units, keep, 0)
-    meet_tiles()
 
     place_of = [order_ref[flip(depth, mask, depth_count), tile] for mask in range(depth_count)]
     ahead = [
@@ -214,8 +202,15 @@
         for i in range(depth_count)
     ]
 
-    def blend(n, carry):
+    def blend(n):
         step = units - 1 - n
+        fetch(step, 0).wait()
+        march(step, 0, own.at[step])
+
+        @pl.when(n == 0)
+        def _():
+            meet_tiles()
+
         for mask in peers:
             if mask:
                 send(step, mask).wait_recv()
@@ -252,9 +247,20 @@
         def _():
             send_row(step, 0).start()
 
+    lag = min(4, units)
+
+    def advance(n, carry):
+        @pl.when(n < units)
+        def _():
+            feed(n)
+
+        @pl.when(n >= lag)
+        def _():
+            blend(n - lag)
+
         return carry
 
-    lax.fori_loop(0, units, blend, 0)
+    lax.fori_loop(0, units + lag, advance, 0)
     here = pl.ds(pl.multiple_of(tile * cols, lanes), cols)
     out_ref[:, :, here] = merged[0, own_place]
 

time: 24.4 us -> 21.3 us (0.87)
  Pallas kernels: 23.5 us -> 20.4 us
    pallas_call x1, Pallas kernels: 23.5 us -> 20.4 us  [local(): pl.pallas_call(functools.partial(kernel, sizes), out_shape=pltpu.VMEM((4,...]
where the time goes in v5:
time: 21.3 us; the launch traced here: 21.1 us
  Pallas kernels  20.4 us (96%)
  local copies, waits for them, and re-layouts  0.71 us (3%)
    pallas_call x1, Pallas kernels, local(): pl.pallas_call(functools.partial(kernel, sizes), out_shape=pltpu.VMEM((4,...  20.4 us
    unnamed x1, local copies, waits for them, and re-layouts  0.71 us

profile of v5, /device:TPU:0, one launch (start us, length us, event | category | flops | bytes accessed | tf_op | source)
XLA Modules:
  0.0 21.1 jit_solution(14870779947774251073)
XLA Ops:
  0.0 20.4 %shard_map.46 = f32[4,8,2048]{2,1,0:T(8,128)S(1)} custom-call(s32[4,8]{1,0:T(4,128)} %bitcast.1, s32[8,256,256]{2,1,0:T(8,128)} %bins_hbm.1, bf16[3,256]{1,0:T(4,128)(2,1)} %colors_ref.1, bf16[256]{0:T(256)(128)(2,1)} %opacity_ref.1), custom_call_target="tpu_custom_call" | custom-call | tf_op jit(solution)/shard_map/pallas_call | solution.py:288
  20.4 0.7 %copy.6 = f32[4,8,2048]{2,1,0:T(8,128)} copy(f32[4,8,2048]{2,1,0:T(8,128)S(1)} %shard_map.46) | data formatting | bytes 524288
